TPU v7x, 32 devices: a whole 2x2x4 slice. The times are simulated.
32 devices in a mesh: seq: 8 (over z, y), tp: 4 (over x, core).
Axes of the slice: x: 2, y: 2, z: 4, core: 2. Of those that a mesh axis runs over, the one named last changes fastest.
Arguments:
- latents: bfloat16 [1024, 3072], P('seq', 'tp'), may hold values from -6 to 6
- lengths: int32 [2], replicated, may hold values from 1 to 768, 1024 in all
- t_index: int32 [2], replicated, may hold values from 0 to 6
- mod_scale: float32 [3072], replicated, may hold values from -2 to 2
- q_weight: bfloat16 [3072, 2048], P(None, 'tp'), may hold values from -0.109375 to 0.109375
- k_weight: bfloat16 [3072, 2048], P(None, 'tp'), may hold values from -0.109375 to 0.109375
- v_weight: bfloat16 [3072, 2048], P(None, 'tp'), may hold values from -0.109375 to 0.109375
- out_weight: bfloat16 [2048, 3072], P('tp'), may hold values from -0.1875 to 0.1875
- q_gain: float32 [128], replicated, may hold values from 0.6 to 2.4
- k_gain: float32 [128], replicated, may hold values from 0.6 to 2.4
- student_weight: bfloat16 [3072, 3072], P('tp'), may hold values from -0.15625 to 0.15625
Outputs:
- target: bfloat16 [1024, 3072], P('seq', 'tp')
- student_velocity: bfloat16 [1024, 3072], P('seq', 'tp')
- loss: float32 [], replicated
Inputs may be any that keep to these rules, and one draw needn't show every extreme that they name: lengths sum to 1024.
All inputs are finite; a program needn't handle non-finite values.
Results may differ from a plain program's by a relative error of at most 0.024.
Values may be sent and summed in bfloat16 or wider, within the bound.
No kernel may reach another device: no remote copies, remote signals or barrier semaphores. Data moves between devices by JAX's collectives and lax.ppermute only.
A program may use at most 64 MiB of HBM per device.

v0:
```python
import math
import jax
import jax.numpy as jnp
from jax import lax
from jax.sharding import PartitionSpec as P

TGRID = 8
epsilon = 1e-06
kinetic_weight = 0.1


def image_index(positions, image_ends):
    return jnp.sum((positions[:, None] >= image_ends[None, :]).astype(jnp.int32), axis=1)


def head_norm(projected, gain):
    shaped = projected.reshape(projected.shape[0], -1, gain.shape[0])
    normed = shaped * lax.rsqrt(jnp.mean(shaped * shaped, axis=-1, keepdims=True) + epsilon) * gain
    return normed.astype(jnp.bfloat16)


def teacher(
    state, times, query_image, image_ends, mod_scale, q_weight, k_weight, v_weight, q_gain, k_gain
):
    row_count = state.shape[0]
    head_dim = q_gain.shape[0]
    state32 = state.astype(jnp.float32)
    normed = state32 * lax.rsqrt(jnp.mean(state32 * state32, axis=1, keepdims=True) + epsilon)
    hidden = (normed * (1.0 + times[:, None] * mod_scale[None, :])).astype(jnp.bfloat16)
    queries = head_norm(jnp.dot(hidden, q_weight, preferred_element_type=jnp.float32), q_gain)
    key_rows = head_norm(jnp.dot(hidden, k_weight, preferred_element_type=jnp.float32), k_gain)
    key_rows = key_rows.reshape(row_count, -1)
    value_rows = jnp.dot(hidden, v_weight, preferred_element_type=jnp.float32).astype(jnp.bfloat16)
    heads_here = queries.shape[1]
    score_scale = 1.0 / math.sqrt(head_dim)

    def attend(carry, key_block, value_block):
        running_max, running_total, running_sum = carry
        count = key_block.shape[0]
        key_image = image_index(jnp.arange(count, dtype=jnp.int32), image_ends)
        key_heads = key_block.reshape(count, heads_here, head_dim)
        value_heads = value_block.reshape(count, heads_here, head_dim)
        same_image = (query_image[:, None] == key_image[None, :])[:, None, :]
        scores = (
            jnp.einsum("qhd,khd->qhk", queries, key_heads, preferred_element_type=jnp.float32)
            * score_scale
        )
        scores = jnp.where(same_image, scores, -1e30)
        new_max = jnp.maximum(running_max, jnp.max(scores, axis=2))
        weights = jnp.where(same_image, jnp.exp(scores - new_max[:, :, None]), 0.0)
        new_total = jnp.sum(weights, axis=2)
        product = jnp.einsum(
            "qhk,khd->qhd",
            weights.astype(jnp.bfloat16),
            value_heads,
            preferred_element_type=jnp.float32,
        )
        return (new_max, new_total, product)

    start_carry = (
        jnp.full((row_count, heads_here), -1e30, jnp.float32),
        jnp.zeros((row_count, heads_here), jnp.float32),
        jnp.zeros((row_count, heads_here, head_dim), jnp.float32),
    )
    offset = jnp.int32(0)
    key_block = lax.all_gather(key_rows, "seq", axis=0, tiled=True)
    value_block = lax.all_gather(value_rows, "seq", axis=0, tiled=True)
    count = key_block.shape[0]
    first_image = image_index(jnp.reshape(offset, (1,)), image_ends)[0]
    last_image = image_index(jnp.reshape(offset + count - 1, (1,)), image_ends)[0]
    touches = jnp.logical_and(first_image <= query_image[-1], last_image >= query_image[0])
    final_max, final_total, final_sum = lax.cond(
        touches,
        lambda inner: attend(inner, key_block, value_block),
        lambda inner: inner,
        start_carry,
    )
    mixed = (final_sum / final_total[:, :, None]).astype(jnp.bfloat16).reshape(row_count, -1)
    return (mixed, hidden)


def on_device(
    latents,
    lengths,
    t_index,
    mod_scale,
    q_weight,
    k_weight,
    v_weight,
    out_weight,
    q_gain,
    k_gain,
    student_weight,
):
    row_count, width_here = latents.shape
    tp_index = lax.axis_index("tp")
    image_ends = jnp.cumsum(lengths)
    row_offset = lax.axis_index("seq") * row_count
    query_image = image_index(row_offset + jnp.arange(row_count, dtype=jnp.int32), image_ends)
    one_hot = (
        query_image[:, None] == jnp.arange(lengths.shape[0], dtype=jnp.int32)[None, :]
    ).astype(jnp.float32)
    start_times = jnp.sum(one_hot * (t_index.astype(jnp.float32) / TGRID)[None, :], axis=1)
    step_size = 1.0 / TGRID
    whole_rows = lax.all_gather(latents, "tp", axis=1, tiled=True)
    velocities = []
    first_hidden = whole_rows
    state_shard = latents
    for euler_index in range(2):
        if euler_index == 1:
            whole_rows = lax.all_gather(state_shard, "tp", axis=1, tiled=True)
        mixed, hidden = teacher(
            whole_rows,
            start_times + euler_index * step_size,
            query_image,
            image_ends,
            mod_scale,
            q_weight,
            k_weight,
            v_weight,
            q_gain,
            k_gain,
        )
        if euler_index == 0:
            first_hidden = hidden
        partial_value = jnp.dot(mixed, out_weight, preferred_element_type=jnp.float32)
        velocity = lax.psum_scatter(
            partial_value.astype(jnp.bfloat16), "tp", scatter_dimension=1, tiled=True
        )
        velocities.append(velocity)
        state_shard = (
            latents.astype(jnp.float32) + step_size * velocity.astype(jnp.float32)
        ).astype(jnp.bfloat16)
    columns = lax.dynamic_slice_in_dim(first_hidden, tp_index * width_here, width_here, 1)
    student_terms = jnp.dot(columns, student_weight, preferred_element_type=jnp.float32)
    student_velocity = lax.psum_scatter(
        student_terms.astype(jnp.bfloat16), "tp", scatter_dimension=1, tiled=True
    )
    target = (0.5 * (velocities[0].astype(jnp.float32) + velocities[1].astype(jnp.float32))).astype(
        jnp.bfloat16
    )
    student32 = student_velocity.astype(jnp.float32)
    residual = student32 - target.astype(jnp.float32)
    per_token = jnp.sum(residual * residual, axis=1) + kinetic_weight * jnp.sum(
        student32 * student32, axis=1
    )
    image_part = jnp.sum(one_hot * per_token[:, None], axis=0)
    image_sum = lax.psum(image_part, ("seq", "tp"))
    loss = jnp.mean(image_sum / (lengths.astype(jnp.float32) * mod_scale.shape[0]))
    return (target, student_velocity, loss)


def solution(mesh):
    placed = (
        P("seq", "tp"),
        P(),
        P(),
        P(),
        P(None, "tp"),
        P(None, "tp"),
        P(None, "tp"),
        P("tp", None),
        P(),
        P(),
        P("tp", None),
    )
    return jax.shard_map(
        on_device,
        mesh=mesh,
        in_specs=placed,
        out_specs=(P("seq", "tp"), P("seq", "tp"), P()),
        check_vma=False,
    )
```

profile of v0, /device:TPU:0, one launch (start us, length us, event | category | flops | bytes accessed | tf_op | source)
XLA Modules:
  0.0 336.3 jit_solution(12734759485271382639)
XLA Ops:
  8.1 10.4 %all_gather.18 = bf16[128,3072]{1,0:T(8,128)(2,1)S(1)} all-gather(bf16[128,768]{1,0:T(8,128)(2,1)} %param.15), channel_id=1, replica_groups=mesh['seq'=8,'tp'=4] {'tp'}, dimensions={1}, use_global_device_ids=true | all-gather | bytes 983040 | tf_op jit(solution)/shard_map/all_gather | solution.py:105
  23.6 3.1 convolution_convert_fusion.4
  26.8 3.4 %fusion.70 = (f32[128,512]{1,0:T(8,128)}, f32[128,512]{1,0:T(8,128)S(1)}) fusion(bf16[128,3072]{1,0:T(8,128)(2,1)} %copy-done.1, bf16[3072,512]{1,0:T(8,128)(2,1)} %param.20), kind=kOutput, calls=%fused_computation.115 | convolution fusion | flops 402718720 | bytes 4456448 | tf_op jit(solution)/shard_map/dot_general | solution.py:31
  30.2 1.8 mul.218
  38.0 2.7 fusion.72
  42.9 25.1 %all-gather.7.cloned.1.call-done = bf16[1024,512]{1,0:T(8,128)(2,1)} async-done(((bf16[128,512]{1,0:T(8,128)(2,1)}), bf16[1024,512]{1,0:T(8,128)(2,1)}) %all-gather.7.cloned.1.call-update) | async-done | bytes 1048592 | tf_op jit(solution)/shard_map/all_gather | solution.py:67
  68.0 41.7 %all-gather.5.cloned.1.call-done = bf16[1024,512]{1,0:T(8,128)(2,1)} async-done(((bf16[128,512]{1,0:T(8,128)(2,1)}), bf16[1024,512]{1,0:T(8,128)(2,1)}) %all-gather.5.cloned.1.call-update) | async-done | bytes 1048592 | tf_op jit(solution)/shard_map/all_gather | solution.py:66
  109.7 6.0 %conditional.2 = (f32[128,4]{0,1:T(4,128)S(1)}, f32[128,4,128]{0,2,1:T(8,128)S(1)}) conditional(s32[]{:T(128)} %convert_element_type.124, () %tuple.24, (s32[128]{0:T(128)S(1)}, s32[2]{0:T(128)}, bf16[1024,512]{1,0:T(8,128)(2,1)}, bf16[128,4,128]{2,0,1:T(8,128)(2,1)S(1)}, bf16[1024,512]{1,0:T(8,128)(2,1)}) %tuple.59), branch_computations={%region_8.9_spmd, %region_9.13_spmd} | conditional | flops 275386880 | bytes 14045748 | solution.py:72
  110.7 1.7 fusion
  117.4 22.0 %reduce-scatter.4.cloned.1.call-done = bf16[128,768]{1,0:T(8,128)(2,1)} async-done(((bf16[128,3072]{1,0:T(8,128)(2,1)}), bf16[128,768]{1,0:T(8,128)(2,1)}) %reduce-scatter.4.cloned.1.call-update) | async-done | bytes 196624 | tf_op jit(solution)/shard_map/reduce_scatter | solution.py:127
  140.4 8.0 %all_gather.21 = bf16[128,3072]{1,0:T(8,128)(2,1)S(1)} all-gather(bf16[128,768]{1,0:T(8,128)(2,1)S(1)} %fusion.43), channel_id=1, replica_groups=mesh['seq'=8,'tp'=4] {'tp'}, dimensions={1}, use_global_device_ids=true | all-gather | bytes 983040 | tf_op jit(solution)/shard_map/all_gather | solution.py:111
  149.3 3.2 convolution_convert_fusion.3
  152.6 3.6 %fusion.71 = (f32[128,512]{1,0:T(8,128)}, f32[128,512]{1,0:T(8,128)}) fusion(bf16[3072,512]{1,0:T(8,128)(2,1)} %param.20, bf16[128,3072]{1,0:T(8,128)(2,1)} %copy-done.3, f32[128]{0:T(128)S(1)} %broadcast_add_fusion, f32[128]{0:T(128)S(1)} %add_rsqrt_fusion.4, f32[3072]{0:T(1024)S(1)} %copy-done.6), kind=kOutput, calls=%fused_computation.116 | convolution fusion | flops 405078016 | bytes 4469760 | tf_op jit(solution)/shard_map/dot_general | solution.py:31
  157.6 1.6 fusion.50
  159.4 4.2 %convolution_convert_fusion.2 = bf16[128,3072]{1,0:T(8,128)(2,1)} fusion(bf16[768,3072]{1,0:T(8,128)(2,1)} %param.25, bf16[128,3072]{1,0:T(8,128)(2,1)} %copy-done.1, s32[]{:T(128)S(6)} %select_n.16), kind=kOutput, calls=%fused_computation.48 | convolution fusion | flops 604372992 | bytes 5701636 | tf_op jit(solution)/shard_map/dot_general | solution.py:135
  163.7 3.5 %fusion.64 = f32[128,512]{1,0:T(8,128)} fusion(bf16[3072,512]{1,0:T(8,128)(2,1)} %param.19, bf16[128,3072]{1,0:T(8,128)(2,1)} %copy-done.3, f32[128]{0:T(128)S(1)} %broadcast_add_fusion, f32[128]{0:T(128)S(1)} %add_rsqrt_fusion.4, f32[3072]{0:T(1024)S(1)} %copy-done.6), kind=kOutput, calls=%fused_computation.112 | convolution fusion | flops 405012480 | bytes 4207616 | tf_op jit(solution)/shard_map/dot_general | solution.py:30
  169.6 23.9 %all-gather.11.cloned.1.call-done = bf16[1024,512]{1,0:T(8,128)(2,1)} async-done(((bf16[128,512]{1,0:T(8,128)(2,1)}), bf16[1024,512]{1,0:T(8,128)(2,1)}) %all-gather.11.cloned.1.call-update) | async-done | bytes 1048592 | tf_op jit(solution)/shard_map/all_gather | solution.py:67
  193.5 41.6 %all-gather.9.cloned.1.call-done = bf16[1024,512]{1,0:T(8,128)(2,1)} async-done(((bf16[128,512]{1,0:T(8,128)(2,1)}), bf16[1024,512]{1,0:T(8,128)(2,1)}) %all-gather.9.cloned.1.call-update) | async-done | bytes 1048592 | tf_op jit(solution)/shard_map/all_gather | solution.py:66
  235.1 5.3 %conditional.3 = (f32[128,4]{0,1:T(4,128)S(1)}, f32[128,4,128]{0,2,1:T(8,128)S(1)}) conditional(s32[]{:T(128)} %convert_element_type.124, () %tuple.26, (s32[128]{0:T(128)S(1)}, s32[2]{0:T(128)S(1)}, bf16[1024,512]{1,0:T(8,128)(2,1)}, bf16[128,4,128]{2,0,1:T(8,128)(2,1)S(1)}, bf16[1024,512]{1,0:T(8,128)(2,1)}) %tuple.60), branch_computations={%region_17.18_spmd, %region_18.0_spmd} | conditional | flops 275386880 | bytes 14045748 | solution.py:72
  235.4 1.8 fusion.18
  242.0 18.1 %reduce-scatter.8.cloned.1.call-done = bf16[128,768]{1,0:T(8,128)(2,1)} async-done(((bf16[128,3072]{1,0:T(8,128)(2,1)}), bf16[128,768]{1,0:T(8,128)(2,1)}) %reduce-scatter.8.cloned.1.call-update) | async-done | bytes 196624 | tf_op jit(solution)/shard_map/reduce_scatter | solution.py:136
  260.0 25.8 %reduce-scatter.6.cloned.1.call-done = bf16[128,768]{1,0:T(8,128)(2,1)} async-done(((bf16[128,3072]{1,0:T(8,128)(2,1)}), bf16[128,768]{1,0:T(8,128)(2,1)}) %reduce-scatter.6.cloned.1.call-update) | async-done | bytes 196624 | tf_op jit(solution)/shard_map/reduce_scatter | solution.py:127
  285.8 1.8 fusion.48
  287.8 39.3 %psum.7 = f32[2]{0:T(128)S(1)} all-reduce(f32[2]{0:T(128)S(1)} %select_reduce_fusion), channel_id=1, replica_groups=mesh['seq'=8,'tp'=4] {'seq','tp'}, use_global_device_ids=true, to_apply=%region_27.28 | all-reduce | flops 2 | bytes 16 | tf_op jit(solution)/shard_map/psum | solution.py:148
  (98 shorter events, 29.2 us)
Async XLA Ops:
  7.2 108.6 %copy-start = (bf16[512,3072]{1,0:T(8,128)(2,1)S(1)}, bf16[512,3072]{1,0:T(8,128)(2,1)}, u32[]{:S(2)}) copy-start(bf16[512,3072]{1,0:T(8,128)(2,1)} %param.22) | copy-start | bytes 9437188
  7.2 60.8 %all-gather.7.cloned.1.call-start = ((), (), s32[]{:S(2)}) async-start(), calls=%async_computation.4 | async-start | bytes 1179648 | tf_op jit(solution)/shard_map/all_gather | solution.py:67
  18.5 0.9 copy-start.2
  20.4 14.4 %copy-start.8 = (s32[2,1]{0,1:T(1,128)}, s32[2,1]{0,1:T(1,128)S(1)}, u32[]{:S(2)}) copy-start(s32[2,1]{0,1:T(1,128)S(1)} %reduce-window.4) | copy-start | bytes 28
  20.6 0.6 copy-start.10
  22.7 0.9 copy-start.1
  26.7 6.4 %copy-start.12 = (f32[128]{0:T(128)S(1)}, f32[128]{0:T(128)}, u32[]{:S(2)}) copy-start(f32[128]{0:T(128)} %param.24) | copy-start | bytes 1540
  26.7 83.0 %all-gather.5.cloned.1.call-start = ((), (), s32[]{:S(2)}) async-start(), calls=%async_computation.3 | async-start | bytes 1179648 | tf_op jit(solution)/shard_map/all_gather | solution.py:66
  34.1 105.3 %reduce-scatter.4.cloned.1.call-start = ((), (), s32[]{:S(2)}) async-start(), calls=%async_computation.5 | async-start | bytes 983040 | tf_op jit(solution)/shard_map/reduce_scatter | solution.py:127
  38.0 4.8 %copy-start.7 = (f32[128]{0:T(128)S(1)}, f32[128]{0:T(128)}, u32[]{:S(2)}) copy-start(f32[128]{0:T(128)} %param.23) | copy-start | bytes 1540
  109.7 2.8 copy-start.14
  115.8 1.6 copy-start.11
  115.8 23.6 %copy-start.5 = (bf16[128,768]{1,0:T(8,128)(2,1)S(1)}, bf16[128,768]{1,0:T(8,128)(2,1)}, u32[]{:S(2)}) copy-start(bf16[128,768]{1,0:T(8,128)(2,1)} %param.15) | copy-start | bytes 589828
  117.3 32.0 %copy-start.6 = (f32[3072]{0:T(1024)S(1)}, f32[3072]{0:T(1024)}, u32[]{:S(2)}) copy-start(f32[3072]{0:T(1024)} %param.18) | copy-start | bytes 36868
  117.3 76.2 %all-gather.11.cloned.1.call-start = ((), (), s32[]{:S(2)}) async-start(), calls=%async_computation.7 | async-start | bytes 1179648 | tf_op jit(solution)/shard_map/all_gather | solution.py:67
  148.4 0.9 copy-start.3
  152.5 82.5 %all-gather.9.cloned.1.call-start = ((), (), s32[]{:S(2)}) async-start(), calls=%async_computation.6 | async-start | bytes 1179648 | tf_op jit(solution)/shard_map/all_gather | solution.py:66
  159.3 100.7 %reduce-scatter.8.cloned.1.call-start = ((), (), s32[]{:S(2)}) async-start(), calls=%async_computation.9 | async-start | bytes 983040 | tf_op jit(solution)/shard_map/reduce_scatter | solution.py:136
  163.6 122.2 %reduce-scatter.6.cloned.1.call-start = ((), (), s32[]{:S(2)}) async-start(), calls=%async_computation.8 | async-start | bytes 983040 | tf_op jit(solution)/shard_map/reduce_scatter | solution.py:127
  163.7 71.4 %copy-start.9 = (s32[2,1]{0,1:T(1,128)S(1)}, s32[2,1]{0,1:T(1,128)}, u32[]{:S(2)}) copy-start(s32[2,1]{0,1:T(1,128)} %copy-done.8) | copy-start | bytes 28
  235.1 2.1 copy-start.13
  240.4 45.4 %copy-start.4 = (bf16[128,768]{1,0:T(8,128)(2,1)S(1)}, bf16[128,768]{1,0:T(8,128)(2,1)}, u32[]{:S(2)}) copy-start(bf16[128,768]{1,0:T(8,128)(2,1)} %reduce-scatter.4.cloned.1.call-done) | copy-start | bytes 589828
  240.4 86.6 %copy-start.15 = (s32[2]{0:T(128)S(1)}, s32[2]{0:T(128)}, u32[]{:S(2)}) copy-start(s32[2]{0:T(128)} %param.16) | copy-start | bytes 28
Sparse Core Ops, SparseCore 0:
  26.8 41.1 all-gather.6
  70.7 38.9 all-gather.4
  117.4 21.9 reduce-scatter.3
  152.6 40.8 all-gather.10
  196.0 38.9 all-gather.8
  238.0 21.9 reduce-scatter.7
  262.5 23.2 reduce-scatter.5
where the time goes:
time: 337 us; the launch traced here: 336 us
  waiting for transfers between devices  198 us (59%)
  blocking collectives  57.7 us (17%)
  matrix products  33.4 us (10%)
  between operations  18.7 us (6%)
  other arithmetic  16.8 us (5%)
  local copies, waits for them, and re-layouts  11 us (3%)
    all_gather x2, waiting for transfers between devices, teacher(): key_block = lax.all_gather(key_rows, 'seq', axis=0, tiled=True)  83.3 us
    all_gather x2, waiting for transfers between devices, teacher(): value_block = lax.all_gather(value_rows, 'seq', axis=0, tiled=True)  49 us
    reduce_scatter x2, waiting for transfers between devices, on_device(): lax.psum_scatter(partial_value.astype(jnp.bfloat16), 'tp', scatter_dimens...  47.8 us
    psum x1, blocking collectives, on_device(): image_sum = lax.psum(image_part, ('seq', 'tp'))  39.3 us
    reduce_scatter x1, waiting for transfers between devices, on_device(): lax.psum_scatter(student_terms.astype(jnp.bfloat16), 'tp', scatter_dimens...  18.1 us
    all_gather x1, blocking collectives, on_device(): whole_rows = lax.all_gather(latents, 'tp', axis=1, tiled=True)  10.4 us
    all_gather x1, blocking collectives, on_device(): whole_rows = lax.all_gather(state_shard, 'tp', axis=1, tiled=True)  8.03 us
    dot_general x2, matrix products, teacher(): jnp.dot(hidden, k_weight, preferred_element_type=jnp.float32)  7.02 us
  transfers between devices with their start and end apart: 7, of which 7 were waited for; matrix products, arithmetic and copies ran while one was open for 11% of the time, Pallas kernels for 0%

commit v1 on v0

--- a/solution.py
+++ b/solution.py
@@ -63,7 +63,12 @@
         jnp.zeros((row_count, heads_here, head_dim), jnp.float32),
     )
     offset = jnp.int32(0)
-    key_block = lax.all_gather(key_rows, "seq", axis=0, tiled=True)
+    ring = [key_rows]
+    for hop in range(7):
+        ring.append(lax.ppermute(ring[-1], "seq", [(dev, (dev + 1) % 8) for dev in range(8)]))
+    key_block = jnp.roll(
+        jnp.concatenate(ring[::-1], axis=0), (lax.axis_index("seq") + 1) * ring[0].shape[0], axis=0
+    )
     value_block = lax.all_gather(value_rows, "seq", axis=0, tiled=True)
     count = key_block.shape[0]
     first_image = image_index(jnp.reshape(offset, (1,)), image_ends)[0]

time: 337 us -> 284 us (0.84)
  waiting for transfers between devices: 198 us -> 127 us
  local copies, waits for them, and re-layouts: 11 us -> 21.5 us
  other arithmetic: 16.8 us -> 20.4 us
    ppermute x0 -> x14, waiting for transfers between devices: none -> 84.9 us  [teacher(): lax.ppermute(ring[-1], 'seq', [(dev, (dev + 1) % 8) for dev in range(8)])]
    all_gather x2 -> x0, waiting for transfers between devices: 83.3 us -> none  [teacher(): key_block = lax.all_gather(key_rows, 'seq', axis=0, tiled=True)]
    all_gather x2, waiting for transfers between devices: 49 us -> 0.01 us  [teacher(): value_block = lax.all_gather(value_rows, 'seq', axis=0, tiled=True)]
    reduce_scatter x1, waiting for transfers between devices: 18.1 us -> 0.02 us  [on_device(): lax.psum_scatter(student_terms.astype(jnp.bfloat16), 'tp', scatter_dimens...]
    unnamed x28 -> x64, local copies, waits for them, and re-layouts: 3.05 us -> 11.2 us
    reduce_scatter x2, waiting for transfers between devices: 47.8 us -> 42.2 us  [on_device(): lax.psum_scatter(partial_value.astype(jnp.bfloat16), 'tp', scatter_dimens...]
  transfers between devices with their start and end apart: 7 -> 19, of which waited for: 7 -> 16; matrix products, arithmetic and copies ran while one was open for 11% -> 17% of each run, Pallas kernels for 0% -> 0%
where the time goes in v1:
time: 284 us; the launch traced here: 283 us
  waiting for transfers between devices  127 us (45%)
  blocking collectives  57.6 us (20%)
  matrix products  33.9 us (12%)
  local copies, waits for them, and re-layouts  21.5 us (8%)
  other arithmetic  20.4 us (7%)
  between operations  18.5 us (7%)
  starting transfers between devices  3.34 us (1%)
    ppermute x14, waiting for transfers between devices, teacher(): lax.ppermute(ring[-1], 'seq', [(dev, (dev + 1) % 8) for dev in range(8)])  84.9 us
    reduce_scatter x2, waiting for transfers between devices, on_device(): lax.psum_scatter(partial_value.astype(jnp.bfloat16), 'tp', scatter_dimens...  42.2 us
    psum x1, blocking collectives, on_device(): image_sum = lax.psum(image_part, ('seq', 'tp'))  39.3 us
    unnamed x64, local copies, waits for them, and re-layouts  11.2 us
    all_gather x1, blocking collectives, on_device(): whole_rows = lax.all_gather(latents, 'tp', axis=1, tiled=True)  10.3 us
    all_gather x1, blocking collectives, on_device(): whole_rows = lax.all_gather(state_shard, 'tp', axis=1, tiled=True)  8.01 us
    dot_general x2, matrix products, teacher(): jnp.dot(hidden, k_weight, preferred_element_type=jnp.float32)  7.03 us
    dot_general x2, matrix products, teacher(): jnp.dot(hidden, v_weight, preferred_element_type=jnp.float32)  6.56 us
  transfers between devices with their start and end apart: 19, of which 16 were waited for; matrix products, arithmetic and copies ran while one was open for 17% of the time, Pallas kernels for 0%

profile of v1, /device:TPU:0, one launch (start us, length us, event | category | flops | bytes accessed | tf_op | source)
XLA Modules:
  0.0 282.6 jit_solution(15101647290203145334)
XLA Ops:
  8.8 10.3 %all_gather.12 = bf16[128,3072]{1,0:T(8,128)(2,1)S(1)} all-gather(bf16[128,768]{1,0:T(8,128)(2,1)} %param.17), channel_id=1, replica_groups=mesh['seq'=8,'tp'=4] {'tp'}, dimensions={1}, use_global_device_ids=true | all-gather | bytes 983040 | tf_op jit(solution)/shard_map/all_gather | solution.py:110
  22.7 3.5 %fusion.70 = (f32[128,512]{1,0:T(8,128)}, f32[128,512]{1,0:T(8,128)S(1)}) fusion(bf16[128,3072]{1,0:T(8,128)(2,1)S(1)} %fusion.38, bf16[3072,512]{1,0:T(8,128)(2,1)} %param.22), kind=kOutput, calls=%fused_computation.135 | convolution fusion | flops 402718720 | bytes 4456448 | tf_op jit(solution)/shard_map/dot_general | solution.py:31
  30.9 7.0 %collective-permute-done = bf16[128,512]{1,0:T(8,128)(2,1)S(1)} collective-permute-done((bf16[128,512]{1,0:T(8,128)(2,1)S(1)}, bf16[128,512]{1,0:T(8,128)(2,1)S(1)}, u32[]{:S(2)}, u32[]{:S(2)}) %collective-permute-start) | collective-permute-done | bytes 131104 | tf_op jit(solution)/shard_map/ppermute | solution.py:68
  38.6 7.7 %collective-permute-done.1 = bf16[128,512]{1,0:T(8,128)(2,1)S(1)} collective-permute-done((bf16[128,512]{1,0:T(8,128)(2,1)S(1)}, bf16[128,512]{1,0:T(8,128)(2,1)S(1)}, u32[]{:S(2)}, u32[]{:S(2)}) %collective-permute-start.1) | collective-permute-done | bytes 131104 | tf_op jit(solution)/shard_map/ppermute | solution.py:68
  46.3 3.4 %convolution_convert_fusion.4 = bf16[128,512]{1,0:T(8,128)(2,1)} fusion(bf16[128,3072]{1,0:T(8,128)(2,1)} %copy-done.1, bf16[3072,512]{1,0:T(8,128)(2,1)} %param.23), kind=kOutput, calls=%fused_computation.64 | convolution fusion | flops 402718720 | bytes 4063232 | tf_op jit(solution)/shard_map/dot_general | solution.py:33
  49.8 4.3 %collective-permute-done.2 = bf16[128,512]{1,0:T(8,128)(2,1)} collective-permute-done((bf16[128,512]{1,0:T(8,128)(2,1)S(1)}, bf16[128,512]{1,0:T(8,128)(2,1)}, u32[]{:S(2)}, u32[]{:S(2)}) %collective-permute-start.2) | collective-permute-done | bytes 131104 | tf_op jit(solution)/shard_map/ppermute | solution.py:68
  57.4 4.7 %collective-permute-done.3 = bf16[128,512]{1,0:T(8,128)(2,1)} collective-permute-done((bf16[128,512]{1,0:T(8,128)(2,1)}, bf16[128,512]{1,0:T(8,128)(2,1)}, u32[]{:S(2)}, u32[]{:S(2)}) %collective-permute-start.3) | collective-permute-done | bytes 131104 | tf_op jit(solution)/shard_map/ppermute | solution.py:68
  70.4 7.9 %collective-permute-done.5 = bf16[128,512]{1,0:T(8,128)(2,1)S(1)} collective-permute-done((bf16[128,512]{1,0:T(8,128)(2,1)}, bf16[128,512]{1,0:T(8,128)(2,1)S(1)}, u32[]{:S(2)}, u32[]{:S(2)}) %collective-permute-start.5) | collective-permute-done | bytes 131104 | tf_op jit(solution)/shard_map/ppermute | solution.py:68
  79.1 8.8 %collective-permute-done.6 = bf16[128,512]{1,0:T(8,128)(2,1)S(1)} collective-permute-done((bf16[128,512]{1,0:T(8,128)(2,1)S(1)}, bf16[128,512]{1,0:T(8,128)(2,1)S(1)}, u32[]{:S(2)}, u32[]{:S(2)}) %collective-permute-start.6) | collective-permute-done | bytes 131104 | tf_op jit(solution)/shard_map/ppermute | solution.py:68
  94.0 5.4 %conditional.2 = (f32[128,4]{0,1:T(4,128)S(1)}, f32[128,4,128]{0,2,1:T(8,128)S(1)}) conditional(s32[]{:T(128)} %convert_element_type.124, () %tuple.25, (s32[128]{0:T(128)S(1)}, s32[2]{0:T(128)S(1)}, bf16[2048,512]{1,0:T(8,128)(2,1)}, bf16[128,4,128]{2,0,1:T(8,128)(2,1)}, bf16[1024,512]{1,0:T(8,128)(2,1)}, /*index=5*/s32[]{:T(128)}) %tuple.61), branch_computations={%region_8.10_spmd, %region_9.14_spmd.clone} | conditional | flops 275386880 | bytes 14046260 | solution.py:77
  101.1 21.7 %reduce-scatter.4.cloned.1.call-done = bf16[128,768]{1,0:T(8,128)(2,1)} async-done(((bf16[128,3072]{1,0:T(8,128)(2,1)}), bf16[128,768]{1,0:T(8,128)(2,1)}) %reduce-scatter.4.cloned.1.call-update) | async-done | bytes 196624 | tf_op jit(solution)/shard_map/reduce_scatter | solution.py:132
  123.9 8.0 %all_gather.14 = bf16[128,3072]{1,0:T(8,128)(2,1)S(1)} all-gather(bf16[128,768]{1,0:T(8,128)(2,1)S(1)} %fusion.43), channel_id=1, replica_groups=mesh['seq'=8,'tp'=4] {'tp'}, dimensions={1}, use_global_device_ids=true | all-gather | bytes 983040 | tf_op jit(solution)/shard_map/all_gather | solution.py:116
  136.0 3.6 %fusion.71 = (f32[128,512]{1,0:T(8,128)}, f32[128,512]{1,0:T(8,128)}) fusion(bf16[3072,512]{1,0:T(8,128)(2,1)} %param.22, bf16[128,3072]{1,0:T(8,128)(2,1)} %copy-done.3, f32[128]{0:T(128)S(1)} %broadcast_add_fusion, f32[128]{0:T(128)S(1)} %add_rsqrt_fusion.4, f32[3072]{0:T(1024)S(1)} %copy-done.12), kind=kOutput, calls=%fused_computation.136 | convolution fusion | flops 405078016 | bytes 4469760 | tf_op jit(solution)/shard_map/dot_general | solution.py:31
  143.6 7.8 %collective-permute-done.7 = bf16[128,512]{1,0:T(8,128)(2,1)S(1)} collective-permute-done((bf16[128,512]{1,0:T(8,128)(2,1)S(1)}, bf16[128,512]{1,0:T(8,128)(2,1)S(1)}, u32[]{:S(2)}, u32[]{:S(2)}) %collective-permute-start.7) | collective-permute-done | bytes 131104 | tf_op jit(solution)/shard_map/ppermute | solution.py:68
  152.1 7.9 %collective-permute-done.8 = bf16[128,512]{1,0:T(8,128)(2,1)S(1)} collective-permute-done((bf16[128,512]{1,0:T(8,128)(2,1)S(1)}, bf16[128,512]{1,0:T(8,128)(2,1)S(1)}, u32[]{:S(2)}, u32[]{:S(2)}) %collective-permute-start.8) | collective-permute-done | bytes 131104 | tf_op jit(solution)/shard_map/ppermute | solution.py:68
  159.9 7.8 %collective-permute-done.9 = bf16[128,512]{1,0:T(8,128)(2,1)S(1)} collective-permute-done((bf16[128,512]{1,0:T(8,128)(2,1)S(1)}, bf16[128,512]{1,0:T(8,128)(2,1)S(1)}, u32[]{:S(2)}, u32[]{:S(2)}) %collective-permute-start.9) | collective-permute-done | bytes 131104 | tf_op jit(solution)/shard_map/ppermute | solution.py:68
  167.8 4.2 %convolution_convert_fusion.2 = bf16[128,3072]{1,0:T(8,128)(2,1)} fusion(bf16[768,3072]{1,0:T(8,128)(2,1)} %param.27, bf16[128,3072]{1,0:T(8,128)(2,1)} %copy-done.1, s32[]{:T(128)S(6)} %select_n.26), kind=kOutput, calls=%fused_computation.50 | convolution fusion | flops 604372992 | bytes 5701636 | tf_op jit(solution)/shard_map/dot_general | solution.py:140
  172.0 4.1 %collective-permute-done.10 = bf16[128,512]{1,0:T(8,128)(2,1)} collective-permute-done((bf16[128,512]{1,0:T(8,128)(2,1)S(1)}, bf16[128,512]{1,0:T(8,128)(2,1)}, u32[]{:S(2)}, u32[]{:S(2)}) %collective-permute-start.10) | collective-permute-done | bytes 131104 | tf_op jit(solution)/shard_map/ppermute | solution.py:68
  176.1 3.5 %fusion.64 = f32[128,512]{1,0:T(8,128)} fusion(bf16[3072,512]{1,0:T(8,128)(2,1)} %param.21, bf16[128,3072]{1,0:T(8,128)(2,1)} %copy-done.3, f32[128]{0:T(128)S(1)} %copy-done.25, f32[128]{0:T(128)} %copy-done.26, f32[3072]{0:T(1024)S(1)} %copy-done.12), kind=kOutput, calls=%fused_computation.132 | convolution fusion | flops 405012480 | bytes 4207616 | tf_op jit(solution)/shard_map/dot_general | solution.py:30
  184.1 7.9 %collective-permute-done.12 = bf16[128,512]{1,0:T(8,128)(2,1)S(1)} collective-permute-done((bf16[128,512]{1,0:T(8,128)(2,1)}, bf16[128,512]{1,0:T(8,128)(2,1)S(1)}, u32[]{:S(2)}, u32[]{:S(2)}) %collective-permute-start.12) | collective-permute-done | bytes 131104 | tf_op jit(solution)/shard_map/ppermute | solution.py:68
  193.7 5.9 %collective-permute-done.13 = bf16[128,512]{1,0:T(8,128)(2,1)S(1)} collective-permute-done((bf16[128,512]{1,0:T(8,128)(2,1)S(1)}, bf16[128,512]{1,0:T(8,128)(2,1)S(1)}, u32[]{:S(2)}, u32[]{:S(2)}) %collective-permute-start.13) | collective-permute-done | bytes 131104 | tf_op jit(solution)/shard_map/ppermute | solution.py:68
  204.9 5.4 %conditional.3 = (f32[128,4]{0,1:T(4,128)S(1)}, f32[128,4,128]{0,2,1:T(8,128)S(1)}) conditional(s32[]{:T(128)} %convert_element_type.124, () %tuple.27, (s32[128]{0:T(128)S(1)}, s32[2]{0:T(128)S(1)}, bf16[2048,512]{1,0:T(8,128)(2,1)}, bf16[128,4,128]{2,0,1:T(8,128)(2,1)}, bf16[1024,512]{1,0:T(8,128)(2,1)}, /*index=5*/s32[]{:T(128)}) %tuple.62), branch_computations={%region_17.19_spmd, %region_18.23_spmd.clone} | conditional | flops 275386880 | bytes 14046260 | solution.py:77
  212.0 20.5 %reduce-scatter.6.cloned.1.call-done = bf16[128,768]{1,0:T(8,128)(2,1)} async-done(((bf16[128,3072]{1,0:T(8,128)(2,1)}), bf16[128,768]{1,0:T(8,128)(2,1)}) %reduce-scatter.6.cloned.1.call-update) | async-done | bytes 196624 | tf_op jit(solution)/shard_map/reduce_scatter | solution.py:132
  234.4 39.3 %psum.7 = f32[2]{0:T(128)S(1)} all-reduce(f32[2]{0:T(128)S(1)} %select_reduce_fusion), channel_id=1, replica_groups=mesh['seq'=8,'tp'=4] {'seq','tp'}, use_global_device_ids=true, to_apply=%region_27.29 | all-reduce | flops 2 | bytes 16 | tf_op jit(solution)/shard_map/psum | solution.py:153
  (160 shorter events, 64.4 us)
Async XLA Ops:
  7.2 92.4 %copy-start = (bf16[512,3072]{1,0:T(8,128)(2,1)S(1)}, bf16[512,3072]{1,0:T(8,128)(2,1)}, u32[]{:S(2)}) copy-start(bf16[512,3072]{1,0:T(8,128)(2,1)} %param.24) | copy-start | bytes 9437188
  7.2 86.9 %all-gather.3.cloned.1.call-start = ((), (), s32[]{:S(2)}) async-start(), calls=%async_computation.3 | async-start | bytes 1179648 | tf_op jit(solution)/shard_map/all_gather | solution.py:72
  21.0 41.1 %copy-start.16 = (s32[2,1]{0,1:T(1,128)}, s32[2,1]{0,1:T(1,128)S(1)}, u32[]{:S(2)}) copy-start(s32[2,1]{0,1:T(1,128)S(1)} %reduce-window.4) | copy-start | bytes 28
  21.1 72.9 %copy-start.13 = (s32[128]{0:T(128)}, s32[128]{0:T(128)S(1)}, u32[]{:S(2)}) copy-start(s32[128]{0:T(128)S(1)} %fusion.58) | copy-start | bytes 1540
  29.3 8.6 %collective-permute-start = (bf16[128,512]{1,0:T(8,128)(2,1)S(1)}, bf16[128,512]{1,0:T(8,128)(2,1)S(1)}, u32[]{:S(2)}, u32[]{:S(2)}) collective-permute-start(bf16[128,512]{1,0:T(8,128)(2,1)S(1)} %fusion.52), channel_id=1, source_target_pairs={{0,4},{4,8},{8,12},{12,16},{16,20},{20,24},{24,28},{28,0},{1,5},{5... | collective-permute-start | bytes 393224 | tf_op jit(solution)/shard_map/ppermute | solution.py:68
  38.6 7.7 %collective-permute-start.1 = (bf16[128,512]{1,0:T(8,128)(2,1)S(1)}, bf16[128,512]{1,0:T(8,128)(2,1)S(1)}, u32[]{:S(2)}, u32[]{:S(2)}) collective-permute-start(bf16[128,512]{1,0:T(8,128)(2,1)S(1)} %collective-permute-done), channel_id=1, source_target_pairs={{0,4},{4,8},{8,12},{12,16},{16,20},{20,24},{24,28},{28,0},{1,5},{5... | collective-permute-start | bytes 393224 | tf_op jit(solution)/shard_map/ppermute | solution.py:68
  46.3 7.8 %collective-permute-start.2 = (bf16[128,512]{1,0:T(8,128)(2,1)S(1)}, bf16[128,512]{1,0:T(8,128)(2,1)}, u32[]{:S(2)}, u32[]{:S(2)}) collective-permute-start(bf16[128,512]{1,0:T(8,128)(2,1)S(1)} %collective-permute-done.1), channel_id=1, source_target_pairs={{0,4},{4,8},{8,12},{12,16},{16,20},{20,24},{24,28},{28,0},{1,5},{5... | collective-permute-start | bytes 393224 | tf_op jit(solution)/shard_map/ppermute | solution.py:68
  49.8 73.1 %reduce-scatter.4.cloned.1.call-start = ((), (), s32[]{:S(2)}) async-start(), calls=%async_computation.4 | async-start | bytes 983040 | tf_op jit(solution)/shard_map/reduce_scatter | solution.py:132
  54.1 8.0 %collective-permute-start.3 = (bf16[128,512]{1,0:T(8,128)(2,1)}, bf16[128,512]{1,0:T(8,128)(2,1)}, u32[]{:S(2)}, u32[]{:S(2)}) collective-permute-start(bf16[128,512]{1,0:T(8,128)(2,1)} %collective-permute-done.2), channel_id=1, source_target_pairs={{0,4},{4,8},{8,12},{12,16},{16,20},{20,24},{24,28},{28,0},{1,5},{5... | collective-permute-start | bytes 393224 | tf_op jit(solution)/shard_map/ppermute | solution.py:68
  62.1 8.3 %collective-permute-start.4 = (bf16[128,512]{1,0:T(8,128)(2,1)}, bf16[128,512]{1,0:T(8,128)(2,1)}, u32[]{:S(2)}, u32[]{:S(2)}) collective-permute-start(bf16[128,512]{1,0:T(8,128)(2,1)} %collective-permute-done.3), channel_id=1, source_target_pairs={{0,4},{4,8},{8,12},{12,16},{16,20},{20,24},{24,28},{28,0},{1,5},{5... | collective-permute-start | bytes 393224 | tf_op jit(solution)/shard_map/ppermute | solution.py:68
  70.4 7.9 %collective-permute-start.5 = (bf16[128,512]{1,0:T(8,128)(2,1)}, bf16[128,512]{1,0:T(8,128)(2,1)S(1)}, u32[]{:S(2)}, u32[]{:S(2)}) collective-permute-start(bf16[128,512]{1,0:T(8,128)(2,1)} %collective-permute-done.4), channel_id=1, source_target_pairs={{0,4},{4,8},{8,12},{12,16},{16,20},{20,24},{24,28},{28,0},{1,5},{5... | collective-permute-start | bytes 393224 | tf_op jit(solution)/shard_map/ppermute | solution.py:68
  78.3 9.6 %collective-permute-start.6 = (bf16[128,512]{1,0:T(8,128)(2,1)S(1)}, bf16[128,512]{1,0:T(8,128)(2,1)S(1)}, u32[]{:S(2)}, u32[]{:S(2)}) collective-permute-start(bf16[128,512]{1,0:T(8,128)(2,1)S(1)} %collective-permute-done.5), channel_id=1, source_target_pairs={{0,4},{4,8},{8,12},{12,16},{16,20},{20,24},{24,28},{28,0},{1,5},{5... | collective-permute-start | bytes 393224 | tf_op jit(solution)/shard_map/ppermute | solution.py:68
  101.1 103.8 %all-gather.5.cloned.1.call-start = ((), (), s32[]{:S(2)}) async-start(), calls=%async_computation.5 | async-start | bytes 1179648 | tf_op jit(solution)/shard_map/all_gather | solution.py:72
  101.1 34.9 %copy-start.24 = (f32[128]{0:T(128)}, f32[128]{0:T(128)S(1)}, u32[]{:S(2)}) copy-start(f32[128]{0:T(128)S(1)} %broadcast_add_fusion) | copy-start | bytes 1540
  136.0 76.0 %reduce-scatter.8.cloned.1.call-start = ((), (), s32[]{:S(2)}) async-start(), calls=%async_computation.7 | async-start | bytes 983040 | tf_op jit(solution)/shard_map/reduce_scatter | solution.py:141
  142.1 9.3 %collective-permute-start.7 = (bf16[128,512]{1,0:T(8,128)(2,1)S(1)}, bf16[128,512]{1,0:T(8,128)(2,1)S(1)}, u32[]{:S(2)}, u32[]{:S(2)}) collective-permute-start(bf16[128,512]{1,0:T(8,128)(2,1)S(1)} %fusion.50), channel_id=1, source_target_pairs={{0,4},{4,8},{8,12},{12,16},{16,20},{20,24},{24,28},{28,0},{1,5},{5... | collective-permute-start | bytes 393224 | tf_op jit(solution)/shard_map/ppermute | solution.py:68
  152.1 7.9 %collective-permute-start.8 = (bf16[128,512]{1,0:T(8,128)(2,1)S(1)}, bf16[128,512]{1,0:T(8,128)(2,1)S(1)}, u32[]{:S(2)}, u32[]{:S(2)}) collective-permute-start(bf16[128,512]{1,0:T(8,128)(2,1)S(1)} %collective-permute-done.7), channel_id=1, source_target_pairs={{0,4},{4,8},{8,12},{12,16},{16,20},{20,24},{24,28},{28,0},{1,5},{5... | collective-permute-start | bytes 393224 | tf_op jit(solution)/shard_map/ppermute | solution.py:68
  159.9 7.8 %collective-permute-start.9 = (bf16[128,512]{1,0:T(8,128)(2,1)S(1)}, bf16[128,512]{1,0:T(8,128)(2,1)S(1)}, u32[]{:S(2)}, u32[]{:S(2)}) collective-permute-start(bf16[128,512]{1,0:T(8,128)(2,1)S(1)} %collective-permute-done.8), channel_id=1, source_target_pairs={{0,4},{4,8},{8,12},{12,16},{16,20},{20,24},{24,28},{28,0},{1,5},{5... | collective-permute-start | bytes 393224 | tf_op jit(solution)/shard_map/ppermute | solution.py:68
  167.8 8.3 %collective-permute-start.10 = (bf16[128,512]{1,0:T(8,128)(2,1)S(1)}, bf16[128,512]{1,0:T(8,128)(2,1)}, u32[]{:S(2)}, u32[]{:S(2)}) collective-permute-start(bf16[128,512]{1,0:T(8,128)(2,1)S(1)} %collective-permute-done.9), channel_id=1, source_target_pairs={{0,4},{4,8},{8,12},{12,16},{16,20},{20,24},{24,28},{28,0},{1,5},{5... | collective-permute-start | bytes 393224 | tf_op jit(solution)/shard_map/ppermute | solution.py:68
  172.0 60.5 %reduce-scatter.6.cloned.1.call-start = ((), (), s32[]{:S(2)}) async-start(), calls=%async_computation.6 | async-start | bytes 983040 | tf_op jit(solution)/shard_map/reduce_scatter | solution.py:132
  176.1 8.0 %collective-permute-start.11 = (bf16[128,512]{1,0:T(8,128)(2,1)}, bf16[128,512]{1,0:T(8,128)(2,1)}, u32[]{:S(2)}, u32[]{:S(2)}) collective-permute-start(bf16[128,512]{1,0:T(8,128)(2,1)} %collective-permute-done.10), channel_id=1, source_target_pairs={{0,4},{4,8},{8,12},{12,16},{16,20},{20,24},{24,28},{28,0},{1,5},{5... | collective-permute-start | bytes 393224 | tf_op jit(solution)/shard_map/ppermute | solution.py:68
  184.1 7.9 %collective-permute-start.12 = (bf16[128,512]{1,0:T(8,128)(2,1)}, bf16[128,512]{1,0:T(8,128)(2,1)S(1)}, u32[]{:S(2)}, u32[]{:S(2)}) collective-permute-start(bf16[128,512]{1,0:T(8,128)(2,1)} %collective-permute-done.11), channel_id=1, source_target_pairs={{0,4},{4,8},{8,12},{12,16},{16,20},{20,24},{24,28},{28,0},{1,5},{5... | collective-permute-start | bytes 393224 | tf_op jit(solution)/shard_map/ppermute | solution.py:68
  191.9 7.7 %collective-permute-start.13 = (bf16[128,512]{1,0:T(8,128)(2,1)S(1)}, bf16[128,512]{1,0:T(8,128)(2,1)S(1)}, u32[]{:S(2)}, u32[]{:S(2)}) collective-permute-start(bf16[128,512]{1,0:T(8,128)(2,1)S(1)} %collective-permute-done.12), channel_id=1, source_target_pairs={{0,4},{4,8},{8,12},{12,16},{16,20},{20,24},{24,28},{28,0},{1,5},{5... | collective-permute-start | bytes 393224 | tf_op jit(solution)/shard_map/ppermute | solution.py:68
  210.4 63.3 %copy-start.23 = (s32[2]{0:T(128)S(1)}, s32[2]{0:T(128)}, u32[]{:S(2)}) copy-start(s32[2]{0:T(128)} %param.18) | copy-start | bytes 28
  (22 other events, 195.3 us)
Sparse Core Ops, SparseCore 0:
  49.9 43.5 all-gather.2
  101.2 21.6 reduce-scatter.3
  136.1 43.9 all-gather.4
  183.1 21.9 reduce-scatter.7
  212.1 20.3 reduce-scatter.5
